TPU v7x, 32 devices: a whole 2x2x4 slice. The times are simulated.
32 devices in a mesh: ctx: 8 (over z, x), heads: 4 (over y, core).
Axes of the slice: x: 2, y: 2, z: 4, core: 2. Of those that a mesh axis runs over, the one named last changes fastest.
Arguments:
- query_rows: bfloat16 [8, 16, 2, 128], P('ctx', 'heads'), may hold values from -6 to 6
- past_keys: bfloat16 [8, 16, 512, 128], P(None, 'heads', 'ctx'), may hold values from -6 to 6
- past_values: bfloat16 [8, 16, 512, 128], P(None, 'heads', 'ctx'), may hold values from -6 to 6
- used_length: int32 [8], replicated, may hold values from 256 to 512
Outputs:
- read: bfloat16 [8, 16, 2, 128], P('ctx', 'heads')
All inputs are finite; a program needn't handle non-finite values.
Results may differ from a plain program's by a relative error of at most 0.0015.
Values may be sent and summed in bfloat16 or wider, within the bound.
A program may use at most 64 MiB of HBM per device.

v0:
```python
import jax
import jax.numpy as jnp
from jax import lax
from jax.sharding import PartitionSpec as P

HEAD_SIZE = 128


def local(query_rows, past_keys, past_values, used_length):
    all_queries = lax.all_gather(query_rows, "ctx", axis=0, tiled=True)
    logit = jnp.einsum(
        "bkgd,bktd->bkgt", all_queries, past_keys, preferred_element_type=jnp.float32
    ) * HEAD_SIZE ** (-0.5)
    positions = lax.axis_index("ctx") * past_keys.shape[2] + jnp.arange(past_keys.shape[2])
    filled = positions[None, :] < used_length[:, None]
    logit = jnp.where(filled[:, None, None, :], logit, -1e30)
    top = jnp.max(logit, axis=-1)
    part = jnp.where(filled[:, None, None, :], jnp.exp(logit - top[..., None]), 0.0)
    weight_sum = jnp.sum(part, axis=-1)
    read_sum = jnp.einsum(
        "bkgt,bktd->bkgd", part, past_values.astype(jnp.float32), precision=lax.Precision.HIGHEST
    )
    tops, sums, parts = (
        lax.all_to_all(top[None], "ctx", split_axis=1, concat_axis=0, tiled=True),
        lax.all_to_all(weight_sum[None], "ctx", split_axis=1, concat_axis=0, tiled=True),
        lax.all_to_all(read_sum[None], "ctx", split_axis=1, concat_axis=0, tiled=True),
    )
    best = jnp.max(tops, axis=0)
    scale = jnp.exp(tops - best)
    weight_own = jnp.sum(sums * scale, axis=0)
    read_own = jnp.sum(parts * scale[..., None], axis=0)
    read = (read_own / weight_own[..., None]).astype(jnp.bfloat16)
    return read


def solution(mesh):
    return jax.shard_map(
        local,
        mesh=mesh,
        in_specs=(
            P("ctx", "heads", None, None),
            P(None, "heads", "ctx", None),
            P(None, "heads", "ctx", None),
            P(),
        ),
        out_specs=P("ctx", "heads", None, None),
        check_vma=False,
    )
```

profile of v0, /device:TPU:0, one launch (start us, length us, event | category | flops | bytes accessed | tf_op | source)
XLA Modules:
  0.0 62.1 jit_solution(10074065572557208397)
XLA Ops:
  0.0 0.0 copy-start
  0.0 0.0 copy-start.1
  0.0 0.7 %copy-done.1 = bf16[1,4,2,128]{3,2,1,0:T(2,128)(2,1)S(1)} copy-done((bf16[1,4,2,128]{3,2,1,0:T(2,128)(2,1)S(1)}, bf16[1,4,2,128]{3,2,1,0:T(2,128)(2,1)}, u32[]{:S(2)}) %copy-start.1) | copy-done | bytes 2072
  0.7 0.0 copy-start.2
  0.8 28.1 %all_gather.3 = bf16[8,4,2,128]{3,1,2,0:T(4,128)(2,1)S(1)} all-gather(bf16[1,4,2,128]{3,1,2,0:T(4,128)(2,1)S(1)} %copy.7), channel_id=1, replica_groups=mesh['ctx'=8,'heads'=4] {'ctx'}, dimensions={0}, use_global_device_ids=true | all-gather | bytes 18432 | tf_op jit(solution)/shard_map/all_gather | solution.py:10
  28.8 0.0 copy-done.2
  28.8 0.1 broadcast_compare_fusion
  28.9 1.5 %fusion.10 = (f32[8,4,2]{2,1,0:T(4,128)S(1)}, f32[8,4,2,64]{3,2,1,0:T(2,128)S(1)}) fusion(bf16[8,4,64,128]{3,2,1,0:T(8,128)(2,1)} %param.5, bf16[8,4,2,128]{3,1,2,0:T(4,128)(2,1)S(1)} %all_gather.3, pred[8,64]{1,0:T(8,128)(4,1)S(1)} %broadcast_compare_fusion), kind=kOutput, calls=%fused_computation.19 | convolution fusion | flops 1060800 | bytes 557824 | tf_op jit(solution)/shard_map/bkgd,bktd->bkgt/dot_general | solution.py:11
  30.4 0.7 %copy.11 = f32[1,8,4,2]{2,3,0,1:T(2,128)} copy(f32[1,8,4,2]{3,2,1,0:T(4,128)S(1)} %bitcast.30) | data formatting | bytes 512 | tf_op jit(solution)/shard_map/broadcast_in_dim | solution.py:24
  31.1 4.0 %all-to-all-start.1 = ((f32[1,8,4,2]{2,3,0,1:T(2,128)}), f32[1,8,4,2]{2,3,0,1:T(2,128)S(1)}, u32[]{:S(2)}, u32[]{:S(2)}) async-start(f32[1,8,4,2]{2,3,0,1:T(2,128)} %copy.11), calls=%async_computation.1 | async-start | bytes 16384 | tf_op jit(solution)/shard_map/all_to_all | solution.py:24
  35.1 0.0 copy-done
  35.1 1.2 %convolution_bitcast_fusion = f32[1,8,4,2,128]{4,3,2,0,1:T(2,128)} fusion(bf16[8,4,64,128]{3,2,1,0:T(8,128)(2,1)S(1)} %copy-done, f32[8,4,2,64]{3,2,1,0:T(2,128)S(1)} %get-tuple-element.6, pred[8,64]{1,0:T(8,128)(4,1)S(1)} %broadcast_compare_fusion, f32[8,4,2]{2,1,0:T(4,128)S(1)} %get-tuple-element.5), kind=kOutput, calls=%fused_computation | convolution fusion | flops 6299648 | bytes 574208 | tf_op jit(solution)/shard_map/bkgt,bktd->bkgd/dot_general | solution.py:20
  36.3 0.2 fusion.8
  36.5 0.7 %copy.15 = f32[1,8,4,2]{2,3,0,1:T(2,128)} copy(f32[1,8,4,2]{3,2,1,0:T(4,128)S(1)} %bitcast.31) | data formatting | bytes 512 | tf_op jit(solution)/shard_map/broadcast_in_dim | solution.py:25
  37.2 4.4 %all-to-all-done.1 = f32[1,8,4,2]{2,3,0,1:T(2,128)S(1)} async-done(((f32[1,8,4,2]{2,3,0,1:T(2,128)}), f32[1,8,4,2]{2,3,0,1:T(2,128)S(1)}, u32[]{:S(2)}, u32[]{:S(2)}) %all-to-all-start.1) | async-done | bytes 288 | tf_op jit(solution)/shard_map/all_to_all | solution.py:24
  41.6 3.3 %all-to-all-start.2 = ((f32[1,8,4,2]{2,3,0,1:T(2,128)}), f32[1,8,4,2]{2,3,0,1:T(2,128)S(1)}, u32[]{:S(2)}, u32[]{:S(2)}) async-start(f32[1,8,4,2]{2,3,0,1:T(2,128)} %copy.15), calls=%async_computation.2 | async-start | bytes 16384 | tf_op jit(solution)/shard_map/all_to_all | solution.py:25
  44.9 0.1 copy.12
  45.0 0.1 fusion.6
  45.1 6.3 %all-to-all-done.2 = f32[1,8,4,2]{2,3,0,1:T(2,128)S(1)} async-done(((f32[1,8,4,2]{2,3,0,1:T(2,128)}), f32[1,8,4,2]{2,3,0,1:T(2,128)S(1)}, u32[]{:S(2)}, u32[]{:S(2)}) %all-to-all-start.2) | async-done | bytes 288 | tf_op jit(solution)/shard_map/all_to_all | solution.py:25
  51.4 3.3 %all-to-all-start = ((f32[1,8,4,2,128]{4,3,2,0,1:T(2,128)}), f32[1,8,4,2,128]{4,3,2,0,1:T(2,128)S(1)}, u32[]{:S(2)}, u32[]{:S(2)}) async-start(f32[1,8,4,2,128]{4,3,2,0,1:T(2,128)} %convolution_bitcast_fusion), calls=%async_computation | async-start | bytes 65536 | tf_op jit(solution)/shard_map/all_to_all | solution.py:26
  54.7 0.1 copy.16
  54.8 0.2 fusion.5
  55.0 0.1 copy.18
  55.1 0.1 copy.13
  55.2 6.2 %all-to-all-done = f32[1,8,4,2,128]{4,3,2,0,1:T(2,128)S(1)} async-done(((f32[1,8,4,2,128]{4,3,2,0,1:T(2,128)}), f32[1,8,4,2,128]{4,3,2,0,1:T(2,128)S(1)}, u32[]{:S(2)}, u32[]{:S(2)}) %all-to-all-start) | async-done | bytes 32800 | tf_op jit(solution)/shard_map/all_to_all | solution.py:26
  61.4 0.1 fusion.1
  61.5 0.7 %fusion.7 = bf16[1,4,2,128]{3,2,1,0:T(2,128)(2,1)} fusion(f32[4,2,128]{2,1,0:T(2,128)S(1)} %fusion.1, f32[4,2]{1,0:T(4,128)S(1)} %copy.18), kind=kLoop, calls=%fused_computation.14 | loop fusion | flops 2048 | bytes 6176 | tf_op jit(solution)/shard_map/convert_element_type | solution.py:32
  (3 shorter events, 0.0 us)
Async XLA Ops:
  0.0 35.1 %copy-start = (bf16[8,4,64,128]{3,2,1,0:T(8,128)(2,1)S(1)}, bf16[8,4,64,128]{3,2,1,0:T(8,128)(2,1)}, u32[]{:S(2)}) copy-start(bf16[8,4,64,128]{3,2,1,0:T(8,128)(2,1)} %param.6) | copy-start | bytes 1572868
  0.0 0.7 %copy-start.1 = (bf16[1,4,2,128]{3,2,1,0:T(2,128)(2,1)S(1)}, bf16[1,4,2,128]{3,2,1,0:T(2,128)(2,1)}, u32[]{:S(2)}) copy-start(bf16[1,4,2,128]{3,2,1,0:T(2,128)(2,1)} %param.4) | copy-start | bytes 6148
  0.7 28.1 %copy-start.2 = (s32[8]{0:T(128)S(1)}, s32[8]{0:T(128)}, u32[]{:S(2)}) copy-start(s32[8]{0:T(128)} %param.7) | copy-start | bytes 100
  31.1 10.5 %all-to-all-start.1 = ((f32[1,8,4,2]{2,3,0,1:T(2,128)}), f32[1,8,4,2]{2,3,0,1:T(2,128)S(1)}, u32[]{:S(2)}, u32[]{:S(2)}) async-start(f32[1,8,4,2]{2,3,0,1:T(2,128)} %copy.11), calls=%async_computation.1 | async-start | bytes 16384 | tf_op jit(solution)/shard_map/all_to_all | solution.py:24
  41.6 9.8 %all-to-all-start.2 = ((f32[1,8,4,2]{2,3,0,1:T(2,128)}), f32[1,8,4,2]{2,3,0,1:T(2,128)S(1)}, u32[]{:S(2)}, u32[]{:S(2)}) async-start(f32[1,8,4,2]{2,3,0,1:T(2,128)} %copy.15), calls=%async_computation.2 | async-start | bytes 16384 | tf_op jit(solution)/shard_map/all_to_all | solution.py:25
  51.4 10.0 %all-to-all-start = ((f32[1,8,4,2,128]{4,3,2,0,1:T(2,128)}), f32[1,8,4,2,128]{4,3,2,0,1:T(2,128)S(1)}, u32[]{:S(2)}, u32[]{:S(2)}) async-start(f32[1,8,4,2,128]{4,3,2,0,1:T(2,128)} %convolution_bitcast_fusion), calls=%async_computation | async-start | bytes 65536 | tf_op jit(solution)/shard_map/all_to_all | solution.py:26
where the time goes:
time: 62.5 us; the launch traced here: 62.1 us
  blocking collectives  28.1 us (45%)
  waiting for transfers between devices  16.8 us (27%)
  starting transfers between devices  10.6 us (17%)
  matrix products  2.71 us (4%)
  local copies, waits for them, and re-layouts  2.59 us (4%)
  other arithmetic  1.32 us (2%)
    all_gather x1, blocking collectives, local(): all_queries = lax.all_gather(query_rows, 'ctx', axis=0, tiled=True)  28.1 us
    all_to_all x1, waiting for transfers between devices, local(): lax.all_to_all(weight_sum[None], 'ctx', split_axis=1, concat_axis=0, tile...  6.27 us
    all_to_all x1, waiting for transfers between devices, local(): lax.all_to_all(read_sum[None], 'ctx', split_axis=1, concat_axis=0, tiled=...  6.17 us
    all_to_all x1, waiting for transfers between devices, local(): lax.all_to_all(top[None], 'ctx', split_axis=1, concat_axis=0, tiled=True)  4.37 us
    all_to_all x1, starting transfers between devices, local(): lax.all_to_all(top[None], 'ctx', split_axis=1, concat_axis=0, tiled=True)  3.97 us
    all_to_all x1, starting transfers between devices, local(): lax.all_to_all(read_sum[None], 'ctx', split_axis=1, concat_axis=0, tiled=...  3.33 us
    all_to_all x1, starting transfers between devices, local(): lax.all_to_all(weight_sum[None], 'ctx', split_axis=1, concat_axis=0, tile...  3.32 us
    dot_general x1, matrix products, local(): jnp.einsum('bkgd,bktd->bkgt', all_queries, past_keys, preferred_element_t...  1.51 us
  transfers between devices with their start and end apart: 3, of which 3 were waited for; matrix products, arithmetic and copies ran while one was open for 4% of the time, Pallas kernels for 0%

commit v1 on v0

--- a/solution.py
+++ b/solution.py
@@ -6,8 +6,35 @@
 HEAD_SIZE = 128
 
 
+def obtain_circles(piece_in, dim_at):
+    piece_in = jnp.moveaxis(piece_in, 0, dim_at)
+    last = piece_in.shape
+    response = piece_in.reshape(
+        *last[:dim_at], last[dim_at] * last[dim_at + 1], *last[dim_at + 2 :]
+    )
+    return response
+
+
+def _change_ports(point, named_axis):
+    v1 = point[None]
+    n_blocks = jax.lax.axis_size(named_axis)
+    for at in range(n_blocks.bit_length() - 1):
+        f_next = 1 << at
+        z = jax.lax.ppermute(v1, named_axis, [(h, h ^ f_next) for h in range(n_blocks)])
+        front = jnp.stack([v1, z])
+        known = jax.lax.axis_index(named_axis) >> at & 1
+        v1 = jnp.where(known == 0, front, front[::-1]).reshape(-1, *point.shape)
+    return v1
+
+
 def local(query_rows, past_keys, past_values, used_length):
-    all_queries = lax.all_gather(query_rows, "ctx", axis=0, tiled=True)
+
+    def _update_units(own_rows, array_axis, chunk):
+        tall = _change_ports(own_rows, chunk)
+        part_next = obtain_circles(tall, array_axis)
+        return part_next
+
+    all_queries = _update_units(query_rows, 0, "ctx")
     logit = jnp.einsum(
         "bkgd,bktd->bkgt", all_queries, past_keys, preferred_element_type=jnp.float32
     ) * HEAD_SIZE ** (-0.5)

time: 62.5 us -> 49.1 us (0.79)
  blocking collectives: 28.1 us -> 0 us
  starting transfers between devices: 10.6 us -> 21 us
  waiting for transfers between devices: 16.8 us -> 21.7 us
  local copies, waits for them, and re-layouts: 2.59 us -> 1.86 us
    all_gather x1 -> x0, blocking collectives: 28.1 us -> none  [local(): all_queries = lax.all_gather(query_rows, 'ctx', axis=0, tiled=True)]
    ppermute x0 -> x3, starting transfers between devices: none -> 8.24 us  [_change_ports(): jax.lax.ppermute(v1, named_axis, [(h, h ^ f_next) for h in range(n_blocks)])]
    ppermute x0 -> x3, waiting for transfers between devices: none -> 4.91 us  [_change_ports(): jax.lax.ppermute(v1, named_axis, [(h, h ^ f_next) for h in range(n_blocks)])]
    all_to_all x1, starting transfers between devices: 3.97 us -> 6.14 us  [local(): lax.all_to_all(top[None], 'ctx', split_axis=1, concat_axis=0, tiled=True)]
    unnamed x7 -> x6, local copies, waits for them, and re-layouts: 0.75 us -> 0.01 us
  transfers between devices with their start and end apart: 3 -> 6, of which waited for: 3 -> 6; matrix products, arithmetic and copies ran while one was open for 4% -> 6% of each run, Pallas kernels for 0% -> 0%
where the time goes in v1:
time: 49.1 us; the launch traced here: 48.8 us
  waiting for transfers between devices  21.7 us (44%)
  starting transfers between devices  21 us (43%)
  matrix products  2.7 us (5%)
  local copies, waits for them, and re-layouts  1.86 us (4%)
  other arithmetic  1.41 us (3%)
    ppermute x3, starting transfers between devices, _change_ports(): jax.lax.ppermute(v1, named_axis, [(h, h ^ f_next) for h in range(n_blocks)])  8.24 us
    all_to_all x1, waiting for transfers between devices, local(): lax.all_to_all(weight_sum[None], 'ctx', split_axis=1, concat_axis=0, tile...  6.27 us
    all_to_all x1, waiting for transfers between devices, local(): lax.all_to_all(read_sum[None], 'ctx', split_axis=1, concat_axis=0, tiled=...  6.17 us
    all_to_all x1, starting transfers between devices, local(): lax.all_to_all(top[None], 'ctx', split_axis=1, concat_axis=0, tiled=True)  6.14 us
    ppermute x3, waiting for transfers between devices, _change_ports(): jax.lax.ppermute(v1, named_axis, [(h, h ^ f_next) for h in range(n_blocks)])  4.91 us
    all_to_all x1, waiting for transfers between devices, local(): lax.all_to_all(top[None], 'ctx', split_axis=1, concat_axis=0, tiled=True)  4.37 us
    all_to_all x1, starting transfers between devices, local(): lax.all_to_all(read_sum[None], 'ctx', split_axis=1, concat_axis=0, tiled=...  3.33 us
    all_to_all x1, starting transfers between devices, local(): lax.all_to_all(weight_sum[None], 'ctx', split_axis=1, concat_axis=0, tile...  3.32 us
  transfers between devices with their start and end apart: 6, of which 6 were waited for; matrix products, arithmetic and copies ran while one was open for 6% of the time, Pallas kernels for 0%

profile of v1, /device:TPU:0, one launch (start us, length us, event | category | flops | bytes accessed | tf_op | source)
XLA Modules:
  0.0 48.8 jit_solution(54542594378320308)
XLA Ops:
  0.0 0.0 copy-start
  0.0 3.0 %collective-permute-start = (bf16[1,1,4,2,128]{4,3,2,1,0:T(2,128)(2,1)}, bf16[1,1,4,2,128]{4,3,2,1,0:T(2,128)(2,1)S(1)}, u32[]{:S(2)}, u32[]{:S(2)}) collective-permute-start(bf16[1,1,4,2,128]{4,3,2,1,0:T(2,128)(2,1)} %bitcast.50), channel_id=1, source_target_pairs={{0,4},{4,0},{8,12},{12,8},{16,20},{20,16},{24,28},{28,24},{1,5},{5... | collective-permute-start | bytes 6152 | tf_op jit(solution)/shard_map/ppermute | solution.py:23
  3.0 0.0 copy-start.1
  3.0 1.8 %collective-permute-done = bf16[1,1,4,2,128]{4,3,2,1,0:T(2,128)(2,1)S(1)} collective-permute-done((bf16[1,1,4,2,128]{4,3,2,1,0:T(2,128)(2,1)}, bf16[1,1,4,2,128]{4,3,2,1,0:T(2,128)(2,1)S(1)}, u32[]{:S(2)}, u32[]{:S(2)}) %collective-permute-start) | collective-permute-done | bytes 2080 | tf_op jit(solution)/shard_map/ppermute | solution.py:23
  4.7 0.0 copy-done.1
  4.8 2.2 %collective-permute-start.1 = (bf16[2,1,4,2,128]{4,3,2,0,1:T(2,128)(2,1)S(1)}, bf16[2,1,4,2,128]{4,3,2,0,1:T(2,128)(2,1)S(1)}, u32[]{:S(2)}, u32[]{:S(2)}) collective-permute-start(bf16[2,1,4,2,128]{4,3,2,0,1:T(2,128)(2,1)S(1)} %get-tuple-element.6), channel_id=1, source_target_pairs={{0,8},{4,12},{8,0},{12,4},{16,24},{20,28},{24,16},{28,20},{1,9},{5... | collective-permute-start | bytes 12296 | tf_op jit(solution)/shard_map/ppermute | solution.py:23
  7.0 1.6 %collective-permute-done.1 = bf16[2,1,4,2,128]{4,3,2,0,1:T(2,128)(2,1)S(1)} collective-permute-done((bf16[2,1,4,2,128]{4,3,2,0,1:T(2,128)(2,1)S(1)}, bf16[2,1,4,2,128]{4,3,2,0,1:T(2,128)(2,1)S(1)}, u32[]{:S(2)}, u32[]{:S(2)}) %collective-permute-start.1) | collective-permute-done | bytes 4128 | tf_op jit(solution)/shard_map/ppermute | solution.py:23
  8.6 0.0 copy-start.2
  8.6 3.1 %collective-permute-start.2 = (bf16[4,1,4,2,128]{4,3,2,0,1:T(2,128)(2,1)S(1)}, bf16[4,1,4,2,128]{4,3,2,0,1:T(2,128)(2,1)S(1)}, u32[]{:S(2)}, u32[]{:S(2)}) collective-permute-start(bf16[4,1,4,2,128]{4,3,2,0,1:T(2,128)(2,1)S(1)} %bitcast.46), channel_id=1, source_target_pairs={{0,16},{4,20},{8,24},{12,28},{16,0},{20,4},{24,8},{28,12},{1,17},{... | collective-permute-start | bytes 24584 | tf_op jit(solution)/shard_map/ppermute | solution.py:23
  11.7 0.0 copy-done.2
  11.7 0.1 broadcast_compare_fusion
  11.8 1.6 %collective-permute-done.2 = bf16[4,1,4,2,128]{4,3,2,0,1:T(2,128)(2,1)S(1)} collective-permute-done((bf16[4,1,4,2,128]{4,3,2,0,1:T(2,128)(2,1)S(1)}, bf16[4,1,4,2,128]{4,3,2,0,1:T(2,128)(2,1)S(1)}, u32[]{:S(2)}, u32[]{:S(2)}) %collective-permute-start.2) | collective-permute-done | bytes 8224 | tf_op jit(solution)/shard_map/ppermute | solution.py:23
  13.4 1.5 %fusion.11 = (f32[8,4,2]{2,1,0:T(4,128)S(1)}, f32[8,4,2,64]{3,2,1,0:T(2,128)S(1)}) fusion(bf16[8,4,2,128]{3,2,1,0:T(2,128)(2,1)S(1)} %bitcast.44, bf16[8,4,64,128]{3,2,1,0:T(8,128)(2,1)} %param.5, pred[8,64]{1,0:T(8,128)(4,1)S(1)} %broadcast_compare_fusion), kind=kOutput, calls=%fused_computation.26 | convolution fusion | flops 1060800 | bytes 557824 | tf_op jit(solution)/shard_map/bkgd,bktd->bkgt/dot_general | solution.py:38
  14.9 0.7 %copy.9 = f32[1,8,4,2]{2,3,0,1:T(2,128)} copy(f32[1,8,4,2]{3,2,1,0:T(4,128)S(1)} %bitcast.43) | data formatting | bytes 512 | tf_op jit(solution)/shard_map/broadcast_in_dim | solution.py:51
  15.6 6.1 %all-to-all-start.1 = ((f32[1,8,4,2]{2,3,0,1:T(2,128)}), f32[1,8,4,2]{2,3,0,1:T(2,128)S(1)}, u32[]{:S(2)}, u32[]{:S(2)}) async-start(f32[1,8,4,2]{2,3,0,1:T(2,128)} %copy.9), calls=%async_computation.1 | async-start | bytes 16384 | tf_op jit(solution)/shard_map/all_to_all | solution.py:51
  21.8 0.0 copy-done
  21.8 1.2 %convolution_bitcast_fusion = f32[1,8,4,2,128]{4,3,2,0,1:T(2,128)} fusion(bf16[8,4,64,128]{3,2,1,0:T(8,128)(2,1)S(1)} %copy-done, f32[8,4,2,64]{3,2,1,0:T(2,128)S(1)} %get-tuple-element.8, pred[8,64]{1,0:T(8,128)(4,1)S(1)} %broadcast_compare_fusion, f32[8,4,2]{2,1,0:T(4,128)S(1)} %get-tuple-element.7), kind=kOutput, calls=%fused_computation | convolution fusion | flops 6299648 | bytes 574208 | tf_op jit(solution)/shard_map/bkgt,bktd->bkgd/dot_general | solution.py:47
  23.0 0.2 fusion.7
  23.2 0.7 %copy.13 = f32[1,8,4,2]{2,3,0,1:T(2,128)} copy(f32[1,8,4,2]{3,2,1,0:T(4,128)S(1)} %bitcast.45) | data formatting | bytes 512 | tf_op jit(solution)/shard_map/broadcast_in_dim | solution.py:52
  23.9 4.4 %all-to-all-done.1 = f32[1,8,4,2]{2,3,0,1:T(2,128)S(1)} async-done(((f32[1,8,4,2]{2,3,0,1:T(2,128)}), f32[1,8,4,2]{2,3,0,1:T(2,128)S(1)}, u32[]{:S(2)}, u32[]{:S(2)}) %all-to-all-start.1) | async-done | bytes 288 | tf_op jit(solution)/shard_map/all_to_all | solution.py:51
  28.3 3.3 %all-to-all-start.2 = ((f32[1,8,4,2]{2,3,0,1:T(2,128)}), f32[1,8,4,2]{2,3,0,1:T(2,128)S(1)}, u32[]{:S(2)}, u32[]{:S(2)}) async-start(f32[1,8,4,2]{2,3,0,1:T(2,128)} %copy.13), calls=%async_computation.2 | async-start | bytes 16384 | tf_op jit(solution)/shard_map/all_to_all | solution.py:52
  31.6 0.1 copy.10
  31.7 0.1 fusion.5
  31.8 6.3 %all-to-all-done.2 = f32[1,8,4,2]{2,3,0,1:T(2,128)S(1)} async-done(((f32[1,8,4,2]{2,3,0,1:T(2,128)}), f32[1,8,4,2]{2,3,0,1:T(2,128)S(1)}, u32[]{:S(2)}, u32[]{:S(2)}) %all-to-all-start.2) | async-done | bytes 288 | tf_op jit(solution)/shard_map/all_to_all | solution.py:52
  38.1 3.3 %all-to-all-start = ((f32[1,8,4,2,128]{4,3,2,0,1:T(2,128)}), f32[1,8,4,2,128]{4,3,2,0,1:T(2,128)S(1)}, u32[]{:S(2)}, u32[]{:S(2)}) async-start(f32[1,8,4,2,128]{4,3,2,0,1:T(2,128)} %convolution_bitcast_fusion), calls=%async_computation | async-start | bytes 65536 | tf_op jit(solution)/shard_map/all_to_all | solution.py:53
  41.4 0.1 copy.14
  41.5 0.2 fusion.4
  41.7 0.1 copy.16
  41.8 0.1 copy.11
  41.9 6.2 %all-to-all-done = f32[1,8,4,2,128]{4,3,2,0,1:T(2,128)S(1)} async-done(((f32[1,8,4,2,128]{4,3,2,0,1:T(2,128)}), f32[1,8,4,2,128]{4,3,2,0,1:T(2,128)S(1)}, u32[]{:S(2)}, u32[]{:S(2)}) %all-to-all-start) | async-done | bytes 32800 | tf_op jit(solution)/shard_map/all_to_all | solution.py:53
  48.0 0.1 fusion.1
  48.1 0.7 %fusion.6 = bf16[1,4,2,128]{3,2,1,0:T(2,128)(2,1)} fusion(f32[4,2,128]{2,1,0:T(2,128)S(1)} %fusion.1, f32[4,2]{1,0:T(4,128)S(1)} %copy.16), kind=kLoop, calls=%fused_computation.19 | loop fusion | flops 2048 | bytes 6176 | tf_op jit(solution)/shard_map/convert_element_type | solution.py:59
  (8 shorter events, 0.1 us)
Async XLA Ops:
  0.0 21.8 %copy-start = (bf16[8,4,64,128]{3,2,1,0:T(8,128)(2,1)S(1)}, bf16[8,4,64,128]{3,2,1,0:T(8,128)(2,1)}, u32[]{:S(2)}) copy-start(bf16[8,4,64,128]{3,2,1,0:T(8,128)(2,1)} %param.6) | copy-start | bytes 1572868
  0.0 4.7 %collective-permute-start = (bf16[1,1,4,2,128]{4,3,2,1,0:T(2,128)(2,1)}, bf16[1,1,4,2,128]{4,3,2,1,0:T(2,128)(2,1)S(1)}, u32[]{:S(2)}, u32[]{:S(2)}) collective-permute-start(bf16[1,1,4,2,128]{4,3,2,1,0:T(2,128)(2,1)} %bitcast.50), channel_id=1, source_target_pairs={{0,4},{4,0},{8,12},{12,8},{16,20},{20,16},{24,28},{28,24},{1,5},{5... | collective-permute-start | bytes 6152 | tf_op jit(solution)/shard_map/ppermute | solution.py:23
  3.0 1.8 %copy-start.1 = (bf16[1,4,2,128]{3,2,1,0:T(2,128)(2,1)S(1)}, bf16[1,4,2,128]{3,2,1,0:T(2,128)(2,1)}, u32[]{:S(2)}) copy-start(bf16[1,4,2,128]{3,2,1,0:T(2,128)(2,1)} %param.4) | copy-start | bytes 6148
  4.8 3.8 %collective-permute-start.1 = (bf16[2,1,4,2,128]{4,3,2,0,1:T(2,128)(2,1)S(1)}, bf16[2,1,4,2,128]{4,3,2,0,1:T(2,128)(2,1)S(1)}, u32[]{:S(2)}, u32[]{:S(2)}) collective-permute-start(bf16[2,1,4,2,128]{4,3,2,0,1:T(2,128)(2,1)S(1)} %get-tuple-element.6), channel_id=1, source_target_pairs={{0,8},{4,12},{8,0},{12,4},{16,24},{20,28},{24,16},{28,20},{1,9},{5... | collective-permute-start | bytes 12296 | tf_op jit(solution)/shard_map/ppermute | solution.py:23
  8.6 3.1 %copy-start.2 = (s32[8]{0:T(128)S(1)}, s32[8]{0:T(128)}, u32[]{:S(2)}) copy-start(s32[8]{0:T(128)} %param.7) | copy-start | bytes 100
  8.6 4.7 %collective-permute-start.2 = (bf16[4,1,4,2,128]{4,3,2,0,1:T(2,128)(2,1)S(1)}, bf16[4,1,4,2,128]{4,3,2,0,1:T(2,128)(2,1)S(1)}, u32[]{:S(2)}, u32[]{:S(2)}) collective-permute-start(bf16[4,1,4,2,128]{4,3,2,0,1:T(2,128)(2,1)S(1)} %bitcast.46), channel_id=1, source_target_pairs={{0,16},{4,20},{8,24},{12,28},{16,0},{20,4},{24,8},{28,12},{1,17},{... | collective-permute-start | bytes 24584 | tf_op jit(solution)/shard_map/ppermute | solution.py:23
  15.6 12.7 %all-to-all-start.1 = ((f32[1,8,4,2]{2,3,0,1:T(2,128)}), f32[1,8,4,2]{2,3,0,1:T(2,128)S(1)}, u32[]{:S(2)}, u32[]{:S(2)}) async-start(f32[1,8,4,2]{2,3,0,1:T(2,128)} %copy.9), calls=%async_computation.1 | async-start | bytes 16384 | tf_op jit(solution)/shard_map/all_to_all | solution.py:51
  28.3 9.8 %all-to-all-start.2 = ((f32[1,8,4,2]{2,3,0,1:T(2,128)}), f32[1,8,4,2]{2,3,0,1:T(2,128)S(1)}, u32[]{:S(2)}, u32[]{:S(2)}) async-start(f32[1,8,4,2]{2,3,0,1:T(2,128)} %copy.13), calls=%async_computation.2 | async-start | bytes 16384 | tf_op jit(solution)/shard_map/all_to_all | solution.py:52
  38.1 10.0 %all-to-all-start = ((f32[1,8,4,2,128]{4,3,2,0,1:T(2,128)}), f32[1,8,4,2,128]{4,3,2,0,1:T(2,128)S(1)}, u32[]{:S(2)}, u32[]{:S(2)}) async-start(f32[1,8,4,2,128]{4,3,2,0,1:T(2,128)} %convolution_bitcast_fusion), calls=%async_computation | async-start | bytes 65536 | tf_op jit(solution)/shard_map/all_to_all | solution.py:53
